TPU v7x, 32 devices: a whole 2x2x4 slice. The times are simulated.
32 devices in a mesh: gx: 4 (over x, core), gy: 8 (over z, y).
Axes of the slice: x: 2, y: 2, z: 4, core: 2. Of those that a mesh axis runs over, the one named last changes fastest.
Arguments:
- emission: bfloat16 [98304, 128], P(('gx', 'gy')), may hold values from -6 to 6
- reflectance: float32 [98304], P(('gx', 'gy')), may hold values from 0.3 to 0.9
- link_blocks: bfloat16 [4608, 256, 256], P(('gx', 'gy')), may hold values from -0.109375 to 0.109375
- link_source: int32 [4608], P(('gx', 'gy')), may hold values from 0 to 11
- link_target: int32 [4608, 1], P(('gx', 'gy')), may hold values from 0 to 31, as said below
- link_slot: int32 [4608], P(('gx', 'gy')), may hold values from 0 to 11
- sensor_cell: int32 [16384, 8], P(('gx', 'gy')), may hold values from 0 to 9215
- sensor_weight: float32 [16384, 8], P(('gx', 'gy')), may hold values from 0 to 0.25
Outputs:
- radiosity: float32 [98304, 128], P(('gx', 'gy'))
- sensor_values: float32 [16384, 128], P(('gx', 'gy'))
Inputs may be any that keep to these rules, and one draw needn't show every extreme that they name: `link_target`: the owner of each block is the device that holds it or one of that device's neighbours (i +- 1, j) or (i, j +- 1) inside the grid of devices, without wrapping. Among the 144 blocks of one device at most 9 name any one neighbour, and some neighbour is named exactly 9 times.
All inputs are finite; a program needn't handle non-finite values.
Results may differ from a plain program's by a relative error of at most 0.0039.
Values may be sent and summed in bfloat16 or wider, within the bound.
A program may use at most 128 MiB of HBM per device.

v0:
```python
import functools

import jax
import jax.numpy as jnp
from jax import lax
from jax.experimental import pallas as pl
from jax.experimental.pallas import tpu as pltpu
from jax.sharding import PartitionSpec as P

P_SIZE = 256
S = 128
SWEEPS = 2
TAPS = 8
MESH = pl.DeviceIdType.MESH
MOVES = (("gy", 1), ("gy", -1), ("gx", 1), ("gx", -1))


def ceil_to(n, m):
    return -(-n // m) * m


def divisor_up_to(n, most):
    return max(d for d in range(1, most + 1) if n % d == 0)


def turned(row, size):
    return jnp.transpose(jnp.broadcast_to(row, (size, row.shape[1])))


def make_tables(target, slot, source, me, cols, dims):
    links, clusters, cap, per_group, groups, lanes = (
        dims["links"], dims["clusters"], dims["cap"], dims["per_group"], dims["groups"], dims["lanes"],
    )
    lane = lax.broadcasted_iota(jnp.int32, (1, lanes), 1)
    ways = 4 * cap
    away = target - me
    group = jnp.where(
        away == 0, 4, jnp.where(away == cols, 2, jnp.where(away == -cols, 3, jnp.where(away == 1, 0, 1)))
    )
    group = jnp.where(lane < links, group, 5)
    base = group * (clusters * lanes)
    key = base + slot * lanes + lane
    key_m = turned(key, lanes)
    rank = jnp.sum(jnp.where((key_m < key) & (key_m >= base), 1, 0), axis=0, keepdims=True)
    place = jnp.where(group == 4, ways + rank, group * cap + rank)
    place = jnp.where(lane < links, place, -1)
    code = lane + lanes * (source + 64 * (slot + 64))
    place_m, code_m = turned(place, lanes), turned(code, lanes)
    wide = lax.broadcasted_iota(jnp.int32, (lanes, lanes), 1)
    found = jnp.sum(jnp.where(place_m == wide, code_m, 0), axis=0, keepdims=True)
    block = found & (lanes - 1)
    rest = found >> (lanes.bit_length() - 1)
    from_cluster = rest & 63
    into = jnp.where(rest >= 4096, (rest >> 6) & 63, -1)
    starts = [w * cap for w in range(4)] + [ways + g * per_group for g in range(groups)]
    ends = starts[1:] + [ways + groups * per_group]
    keep = into == pltpu.roll(jnp.broadcast_to(into, (8, lanes)), 1, 1)[0:1]
    for start in starts:
        keep = keep & (lane != start)
    keep = jnp.where(keep & (into >= 0), 1, 0)
    into_m = turned(into, lanes)
    order = lax.broadcasted_iota(jnp.int32, (lanes, lanes), 0)
    first = jnp.zeros((1, lanes), jnp.int32)
    end = jnp.zeros((1, lanes), jnp.int32)
    cluster = jnp.full((1, lanes), -2, jnp.int32)
    for g in range(4 + groups):
        inside = (lane >= g * clusters) & (lane < (g + 1) * clusters)
        first = jnp.where(inside, starts[g], first)
        end = jnp.where(inside, ends[g], end)
        cluster = jnp.where(inside, lane - g * clusters, cluster)
    hit = (into_m == cluster) & (order >= first) & (order < end)
    last = jnp.max(jnp.where(hit, order - first + 1, 0), axis=0, keepdims=True)
    row = lax.broadcasted_iota(jnp.int32, (8, lanes), 0)
    return jnp.where(row == 0, block, jnp.where(row == 1, from_cluster, jnp.where(row == 2, keep, last)))


def fused_kernel(
    target, slot, source, cells, weights, reflect, emission_hbm, blocks_hbm,
    rad_hbm, values,
    blocks, emission, rounded, rad, refl, acc, running, arrived, sends, recvs, item_cell, item_weight, from_cell,
    from_weight, sensor_w, final_t, sum_send, sum_recv, sum_own, table, table_in, table_s, table_in_s,
    load_sem, table_sem, small_send, small_recv, term_send, term_recv, sum_ssem, sum_rsem,
    *, dims,
):
    clusters, cap, per_group, groups = dims["clusters"], dims["cap"], dims["per_group"], dims["groups"]
    unroll, chunks, loads, sensors = dims["unroll"], dims["chunks"], dims["loads"], dims["sensors"]
    rows, links, lanes = dims["rows"], dims["links"], dims["lanes"]
    ways = 4 * cap
    per_chunk = cap // chunks
    wide = dims["wide"]
    pieces = sensors // wide
    i, j = lax.axis_index("gx"), lax.axis_index("gy")
    n_gx, n_gy = lax.axis_size("gx"), lax.axis_size("gy")
    me = i * n_gy + j

    def there(way, back=False):
        axis, step = MOVES[way]
        step = -step if back else step
        at = (j if axis == "gy" else i) + step
        inside = (at >= 0) & (at < (n_gy if axis == "gy" else n_gx))
        return inside, ((i, at) if axis == "gy" else (at, j))

    def remote(src, dst, send, recv, way):
        return pltpu.make_async_remote_copy(
            src_ref=src, dst_ref=dst, send_sem=send, recv_sem=recv, device_id=there(way)[1], device_id_type=MESH
        )

    def if_to(way, act):
        pl.when(there(way)[0])(act)

    def if_from(way, act):
        pl.when(there(way, back=True)[0])(act)

    share = links // loads
    reads = [
        pltpu.make_async_copy(emission_hbm, emission, load_sem.at[loads]),
        pltpu.make_async_copy(emission_hbm, rounded, load_sem.at[loads + 1]),
    ] + [
        pltpu.make_async_copy(blocks_hbm.at[pl.ds(n * share, share)], blocks.at[pl.ds(n * share, share)], load_sem.at[n])
        for n in range(loads)
    ]
    for read in reads:
        read.start()

    barrier = pltpu.get_barrier_semaphore()
    for way in range(4):
        if_to(way, lambda way=way: pl.semaphore_signal(barrier, 1, device_id=there(way)[1], device_id_type=MESH))

    table[...] = make_tables(target[...], slot[...], source[...], me, n_gy, dims)
    table_copy = pltpu.make_async_copy(table, table_s, table_sem.at[0])
    table_copy.start()

    pl.semaphore_wait(barrier, sum(jnp.where(there(way)[0], 1, 0) for way in range(4)))

    def table_send(way):
        return remote(table, table_in.at[way], small_send.at[0, way], small_recv.at[0, way], way)

    def cell_send(way):
        return remote(cells, from_cell.at[way], small_send.at[1, way], small_recv.at[1, way], way)

    def weight_send(way):
        return remote(weights, from_weight.at[way], small_send.at[2, way], small_recv.at[2, way], way)

    for way in range(4):
        if_to(way, lambda way=way: table_send(way).start())
    for way in range(2):
        if_to(way, lambda way=way: cell_send(way).start())
        if_to(way, lambda way=way: weight_send(way).start())

    def spread(t, carry):
        at = pl.ds(pl.multiple_of(t * 128, 128), 128)
        refl[at, :] = turned(reflect[pl.ds(t, 1), :], 128)
        return carry

    lax.fori_loop(0, rows // 128, spread, 0)

    running[0] = jnp.zeros((P_SIZE, S), jnp.float32)
    for way in range(4):
        arrived[way, 0] = jnp.zeros((P_SIZE, S), jnp.float32)

        @pl.when(jnp.logical_not(there(way, back=True)[0]))
        def _(way=way):
            table_in[way] = jnp.zeros(table_in.shape[1:], jnp.int32)
            if way < 2:
                from_cell[way] = jnp.full(from_cell.shape[1:], -1, jnp.int32)
                from_weight[way] = jnp.zeros(from_weight.shape[1:], jnp.float32)
                sum_recv[way] = jnp.zeros(sum_recv.shape[1:], sum_recv.dtype)

    for way in range(4):
        if_from(way, lambda way=way: table_send(way).wait_recv())
    table_in_copy = pltpu.make_async_copy(table_in, table_in_s, table_sem.at[1])
    table_in_copy.start()
    for way in range(2):
        if_from(way, lambda way=way: cell_send(way).wait_recv())
        if_from(way, lambda way=way: weight_send(way).wait_recv())

    for part in range(3):
        cell = cells[...] if part == 2 else from_cell[part]
        weight = weights[...] if part == 2 else from_weight[part]
        total = weight
        for turn in range(1, TAPS):
            total = total + jnp.where(
                cell == pltpu.roll(cell, turn, 0), pltpu.roll(weight, turn, 0), jnp.zeros_like(weight)
            )
        item_cell[part] = cell - (2 * rows, 0, rows)[part]
        item_weight[part] = total

    table_copy.wait()
    table_in_copy.wait()
    for read in reads:
        read.wait()

    def product(q):
        return jnp.dot(blocks[table_s[0, q]], rounded[table_s[1, q]], preferred_element_type=jnp.float32)

    def term_copy(sweep, way, chunk):
        at = pl.ds(way * cap + chunk * per_chunk, per_chunk)
        return remote(
            sends.at[sweep, at], recvs.at[sweep, at], term_send.at[sweep, way, chunk], term_recv.at[sweep, way, chunk], way
        )

    def send_terms(sweep, pair):
        def body(chunk, carry):
            for way in pair:
                for r in range(per_chunk):
                    q = way * cap + chunk * per_chunk + r
                    sends[sweep, q] = product(q).astype(jnp.bfloat16)
            for way in pair:
                if_to(way, lambda way=way: term_copy(sweep, way, chunk).start())
            return carry

        lax.fori_loop(0, chunks, body, 0)

    def stay():
        def group(g, carry):
            def body(t, carry):
                at = t * unroll
                for u in range(unroll):
                    q = ways + g * per_group + at + u
                    held = jnp.where(table_s[2, q] != 0, running[at + u], 0.0)
                    running[at + u + 1] = product(q) + held
                return carry

            lax.fori_loop(0, per_group // unroll, body, 0)

            def into(c, carry):
                acc[c] += running[table_s[3, (4 + g) * clusters + c]]
                return carry

            lax.fori_loop(0, clusters, into, 0)
            return carry

        lax.fori_loop(0, groups, group, 0)

    def receive(sweep, pair):
        def body(chunk, carry):
            for way in pair:
                def scan(way=way):
                    term_copy(sweep, way, chunk).wait_recv()
                    for r in range(per_chunk):
                        n = chunk * per_chunk + r
                        held = jnp.where(table_in_s[way, 2, way * cap + n] != 0, arrived[way, n], 0.0)
                        arrived[way, n + 1] = recvs[sweep, way * cap + n].astype(jnp.float32) + held

                if_from(way, scan)
            return carry

        lax.fori_loop(0, chunks, body, 0)

    def taken(way, c):
        return arrived[way, table_in_s[way, 3, way * clusters + c]]

    tile = 16
    block_rows = 8 * tile
    columns = 3 * sensors // 128
    per_wide = wide // 128

    def sensor_weights(first, count):
        near = lax.broadcasted_iota(jnp.int32, (tile, 128), 0)

        def column(n, carry):
            part = n // (sensors // 128)
            at = pl.ds(pl.multiple_of((n - part * (sensors // 128)) * 128, 128), 128)
            cell = [
                jnp.broadcast_to(item_cell[part, k : k + 1, at], (tile, 128)).astype(jnp.int16) for k in range(TAPS)
            ]
            weight = [
                jnp.broadcast_to(item_weight[part, k : k + 1, at], (tile, 128)).astype(jnp.bfloat16)
                for k in range(TAPS)
            ]
            to = pl.ds(pl.multiple_of((n - (n // per_wide) * per_wide) * 128, 128), 128)

            def body(t, carry):
                for h in range(8):
                    row = pl.multiple_of(t * block_rows + h * tile, tile)
                    here = (near + row).astype(jnp.int16)
                    total = jnp.zeros((tile, 128), jnp.bfloat16)
                    for k in range(TAPS):
                        total = jnp.where(cell[k] == here, weight[k], total)
                    sensor_w[n // per_wide, pl.ds(row, tile), to] = total
                return carry

            lax.fori_loop(0, rows // block_rows, body, 0)
            return carry

        lax.fori_loop(first, first + count, column, 0)

    def sweep_body(sweep, carry):
        send_terms(sweep, (0, 1))
        send_terms(sweep, (2, 3))
        acc[...] = jnp.zeros(acc.shape, jnp.float32)
        stay()
        sensor_weights(sweep * (columns // SWEEPS), columns // SWEEPS)
        receive(sweep, (2, 3))

        def add_x(c, carry):
            acc[c] += taken(2, c) + taken(3, c)
            return carry

        lax.fori_loop(0, clusters, add_x, 0)
        receive(sweep, (0, 1))

        def finish(c, carry):
            at = pl.ds(pl.multiple_of(c * P_SIZE, P_SIZE), P_SIZE)
            incoming = acc[c] + taken(0, c) + taken(1, c)
            value = emission[c].astype(jnp.float32) + refl[at, :] * incoming
            rounded[c] = value.astype(jnp.bfloat16)
            rad[c] = value
            final_t[:, at] = jnp.transpose(value).astype(jnp.bfloat16)
            return carry

        lax.fori_loop(0, clusters, finish, 0)
        return carry

    lax.fori_loop(0, SWEEPS, sweep_body, 0)

    write = pltpu.make_async_copy(rad, rad_hbm, load_sem.at[0])
    write.start()

    def sum_copy(way, piece):
        return remote(
            sum_send.at[way, piece], sum_recv.at[way, piece], sum_ssem.at[way, piece], sum_rsem.at[way, piece], way
        )

    def sums(part, piece):
        return jnp.dot(final_t[...], sensor_w[part * pieces + piece], preferred_element_type=jnp.float32)

    for piece in range(pieces):
        for part in range(2):
            way = 1 - part
            sum_send[way, piece] = sums(part, piece).astype(jnp.bfloat16)
            if_to(way, lambda: sum_copy(way, piece).start())
    for piece in range(pieces):
        sum_own[piece] = sums(2, piece)
    for piece in range(pieces):
        for way in range(2):
            if_from(way, lambda: sum_copy(way, piece).wait_recv())
        total = sum_own[piece] + sum_recv[0, piece].astype(jnp.float32) + sum_recv[1, piece].astype(jnp.float32)
        values[piece * wide : (piece + 1) * wide, :] = jnp.transpose(total)

    write.wait()
    for way in range(4):
        if_to(way, lambda way=way: table_send(way).wait_send())
        for sweep in range(SWEEPS):
            for chunk in range(chunks):
                if_to(way, lambda: term_copy(sweep, way, chunk).wait_send())
    for way in range(2):
        if_to(way, lambda way=way: cell_send(way).wait_send())
        if_to(way, lambda way=way: weight_send(way).wait_send())
        for piece in range(pieces):
            if_to(way, lambda: sum_copy(way, piece).wait_send())


def per_device(
    emission,
    reflectance,
    link_blocks,
    link_source,
    link_target,
    link_slot,
    sensor_cell,
    sensor_weight,
):
    links = link_blocks.shape[0]
    rows = emission.shape[0]
    clusters = rows // P_SIZE
    sensors = sensor_cell.shape[0]
    cap = max(2, links // 16)
    groups = 4 if links % 4 == 0 else 1
    per_group = links // groups
    lanes = 1 << (max(ceil_to(4 * cap + links, 128), ceil_to((4 + groups) * clusters, 128)) - 1).bit_length()
    wide = 256 if sensors % 256 == 0 else 128
    dims = dict(
        links=links, rows=rows, clusters=clusters, sensors=sensors, cap=cap, groups=groups, per_group=per_group,
        lanes=lanes, wide=wide, unroll=divisor_up_to(per_group, 12), chunks=3 if cap % 3 == 0 else 1,
        loads=divisor_up_to(links, 8),
    )
    full = (clusters, P_SIZE, S)
    term = (P_SIZE, S)
    chunks, pieces = dims["chunks"], sensors // wide

    def as_row(x):
        return jnp.pad(x.reshape(1, links), ((0, 0), (0, lanes - links)))

    vmem = pl.BlockSpec(memory_space=pltpu.VMEM)
    hbm = pl.BlockSpec(memory_space=pl.ANY)
    dma = pltpu.SemaphoreType.DMA
    scratch = [
        pltpu.VMEM((links, P_SIZE, P_SIZE), jnp.bfloat16),
        pltpu.VMEM(full, jnp.bfloat16),
        pltpu.VMEM(full, jnp.bfloat16),
        pltpu.VMEM(full, jnp.float32),
        pltpu.VMEM((rows, S), jnp.float32),
        pltpu.VMEM(full, jnp.float32),
        pltpu.VMEM((per_group + 1, *term), jnp.float32),
        pltpu.VMEM((4, cap + 1, *term), jnp.float32),
        pltpu.VMEM((SWEEPS, 4 * cap, *term), jnp.bfloat16),
        pltpu.VMEM((SWEEPS, 4 * cap, *term), jnp.bfloat16),
        pltpu.VMEM((3, TAPS, sensors), jnp.int32),
        pltpu.VMEM((3, TAPS, sensors), jnp.float32),
        pltpu.VMEM((2, TAPS, sensors), jnp.int32),
        pltpu.VMEM((2, TAPS, sensors), jnp.float32),
        pltpu.VMEM((3 * pieces, rows, wide), jnp.bfloat16),
        pltpu.VMEM((S, rows), jnp.bfloat16),
        pltpu.VMEM((2, pieces, S, wide), jnp.bfloat16),
        pltpu.VMEM((2, pieces, S, wide), jnp.bfloat16),
        pltpu.VMEM((pieces, S, wide), jnp.float32),
        pltpu.VMEM((8, lanes), jnp.int32),
        pltpu.VMEM((4, 8, lanes), jnp.int32),
        pltpu.SMEM((8, lanes), jnp.int32),
        pltpu.SMEM((4, 8, lanes), jnp.int32),
        dma((dims["loads"] + 2,)),
        dma((2,)),
        dma((3, 4)),
        dma((3, 4)),
        dma((SWEEPS, 4, chunks)),
        dma((SWEEPS, 4, chunks)),
        dma((2, pieces)),
        dma((2, pieces)),
    ]
    radiosity, values = pl.pallas_call(
        functools.partial(fused_kernel, dims=dims),
        out_shape=[jax.ShapeDtypeStruct(full, jnp.float32), jax.ShapeDtypeStruct((sensors, S), jnp.float32)],
        in_specs=[vmem] * 6 + [hbm] * 2,
        out_specs=[hbm, vmem],
        scratch_shapes=scratch,
        compiler_params=pltpu.CompilerParams(collective_id=0, has_side_effects=True, vmem_limit_bytes=62 * 2**20),
        name="radiosity",
    )(
        as_row(link_target[:, 0]),
        as_row(link_slot),
        as_row(link_source),
        sensor_cell.T,
        sensor_weight.T,
        reflectance.reshape(rows // 128, 128),
        emission.reshape(full),
        link_blocks,
    )
    return radiosity.reshape(rows, S), values


def solution(mesh):
    both = ("gx", "gy")
    return jax.shard_map(
        per_device,
        mesh=mesh,
        in_specs=(
            P(both, None),
            P(both),
            P(both, None, None),
            P(both),
            P(both, None),
            P(both),
            P(both, None),
            P(both, None),
        ),
        out_specs=(P(both, None), P(both, None)),
        check_vma=False,
    )
```

profile of v0, /device:TPU:18, one launch (start us, length us, event | category | flops | bytes accessed | tf_op | source)
XLA Modules:
  0.0 82.8 jit_solution(16368528012809602442)
XLA Ops:
  0.6 1.3 %pad.12.source = s32[1,256]{1,0:T(1,128)} pad(s32[1,144]{1,0:T(1,128)} %bitcast.13, s32[]{:T(128)} %constant.0.clone.1), padding=0_0x0_112 | pad | bytes 1604 | tf_op jit(solution)/shard_map/jit(_pad)/pad | solution.py:383
  1.9 1.2 %pad.10.target = s32[1,256]{1,0:T(1,128)} pad(s32[1,144]{1,0:T(1,128)} %bitcast.14, s32[]{:T(128)} %constant.0.clone.1), padding=0_0x0_112 | pad | bytes 1604 | tf_op jit(solution)/shard_map/jit(_pad)/pad | solution.py:383
  3.1 1.2 %pad.11.slot = s32[1,256]{1,0:T(1,128)} pad(s32[1,144]{1,0:T(1,128)} %bitcast.15, s32[]{:T(128)} %constant.0.clone.1), padding=0_0x0_112 | pad | bytes 1604 | tf_op jit(solution)/shard_map/jit(_pad)/pad | solution.py:383
  4.4 75.0 %radiosity.1 = (f32[12,256,128]{2,1,0:T(8,128)}, f32[512,128]{1,0:T(8,128)}) custom-call(s32[1,256]{1,0:T(1,128)} %pad.10.target, s32[1,256]{1,0:T(1,128)} %pad.11.slot, s32[1,256]{1,0:T(1,128)} %pad.12.source, s32[8,512]{1,0:T(8,128)} %bitcast.10, f32[8,512]{1,0:T(8,128)} %bitcast.11, f32[24,128]{1,0:T(8,128)} %bitcast.12, bf16[12,256,128]{2,1,0:T(8,128)(2,1)} %bitcast.9, ...), custom_call_target="tpu_custom_call" | custom-call | tf_op jit(solution)/shard_map/radiosity/pallas_call | solution.py:421
  79.4 0.0 copy-start
  79.4 2.7 %copy.12 = f32[3072,128]{1,0:T(8,128)} copy(f32[3072,128]{1,0:T(8,128)} %bitcast.8) | data formatting | bytes 3145728
  82.1 0.0 copy-done
  82.1 0.7 copy.13
Async XLA Ops:
  79.4 2.7 %copy-start = (f32[512,128]{1,0:T(8,128)S(1)}, f32[512,128]{1,0:T(8,128)}, u32[]{:S(2)}) copy-start(f32[512,128]{1,0:T(8,128)} %get-tuple-element.9) | copy-start | bytes 786436
where the time goes:
time: 83.1 us; the launch traced here: 82.8 us
  Pallas kernels  75 us (90%)
  local copies, waits for them, and re-layouts  7.16 us (9%)
    pallas_call x1, Pallas kernels, per_device(): pl.pallas_call(functools.partial(fused_kernel, dims=dims), out_shape=[jax...  75 us
    pad x3, local copies, waits for them, and re-layouts, as_row(): return jnp.pad(x.reshape(1, links), ((0, 0), (0, lanes - links)))  3.76 us
    unnamed x4, local copies, waits for them, and re-layouts  3.4 us

commit v1 on v0

--- a/solution.py
+++ b/solution.py
@@ -76,9 +76,9 @@
 
 def fused_kernel(
     target, slot, source, cells, weights, reflect, emission_hbm, blocks_hbm,
-    rad_hbm, values,
-    blocks, emission, rounded, rad, refl, acc, running, arrived, sends, recvs, item_cell, item_weight, from_cell,
-    from_weight, sensor_w, final_t, sum_send, sum_recv, sum_own, table, table_in, table_s, table_in_s,
+    rad_hbm, sum_own,
+    blocks, emission, rounded, crossed, rad, refl, acc, running, arrived, sends, recvs, item_cell, item_weight, from_cell,
+    from_weight, sensor_w, final_t, sum_send, sum_recv, link_rows, table, table_in, table_s, table_in_s,
     load_sem, table_sem, small_send, small_recv, term_send, term_recv, sum_ssem, sum_rsem,
     *, dims,
 ):
@@ -89,6 +89,7 @@
     per_chunk = cap // chunks
     wide = dims["wide"]
     pieces = sensors // wide
+    half_rows, half_cols = P_SIZE // 2, S // 2
     i, j = lax.axis_index("gx"), lax.axis_index("gy")
     n_gx, n_gy = lax.axis_size("gx"), lax.axis_size("gy")
     me = i * n_gy + j
@@ -115,18 +116,22 @@
     reads = [
         pltpu.make_async_copy(emission_hbm, emission, load_sem.at[loads]),
         pltpu.make_async_copy(emission_hbm, rounded, load_sem.at[loads + 1]),
-    ] + [
+    ]
+    block_reads = [
         pltpu.make_async_copy(blocks_hbm.at[pl.ds(n * share, share)], blocks.at[pl.ds(n * share, share)], load_sem.at[n])
         for n in range(loads)
     ]
-    for read in reads:
+    for read in reads + block_reads:
         read.start()
 
     barrier = pltpu.get_barrier_semaphore()
     for way in range(4):
         if_to(way, lambda way=way: pl.semaphore_signal(barrier, 1, device_id=there(way)[1], device_id_type=MESH))
 
-    table[...] = make_tables(target[...], slot[...], source[...], me, n_gy, dims)
+    link_rows[...] = jnp.zeros(link_rows.shape, jnp.int32)
+    for n, link in enumerate((target, slot, source)):
+        link_rows[n, :, 0:links] = link[...]
+    table[...] = make_tables(link_rows[0], link_rows[1], link_rows[2], me, n_gy, dims)
     table_copy = pltpu.make_async_copy(table, table_s, table_sem.at[0])
     table_copy.start()
 
@@ -156,7 +161,7 @@
 
     running[0] = jnp.zeros((P_SIZE, S), jnp.float32)
     for way in range(4):
-        arrived[way, 0] = jnp.zeros((P_SIZE, S), jnp.float32)
+        arrived[way, 0] = jnp.zeros(arrived.shape[2:], jnp.float32)
 
         @pl.when(jnp.logical_not(there(way, back=True)[0]))
         def _(way=way):
@@ -165,6 +170,15 @@
                 from_cell[way] = jnp.full(from_cell.shape[1:], -1, jnp.int32)
                 from_weight[way] = jnp.zeros(from_weight.shape[1:], jnp.float32)
                 sum_recv[way] = jnp.zeros(sum_recv.shape[1:], sum_recv.dtype)
+
+    for read in reads:
+        read.wait()
+
+    def cross(c, carry):
+        crossed[c] = pltpu.roll(emission[c].astype(jnp.float32), half_cols, 1).astype(jnp.bfloat16)
+        return carry
+
+    lax.fori_loop(0, clusters, cross, 0)
 
     for way in range(4):
         if_from(way, lambda way=way: table_send(way).wait_recv())
@@ -187,31 +201,47 @@
 
     table_copy.wait()
     table_in_copy.wait()
-    for read in reads:
+    for read in block_reads:
         read.wait()
 
-    def product(q):
-        return jnp.dot(blocks[table_s[0, q]], rounded[table_s[1, q]], preferred_element_type=jnp.float32)
-
-    def term_copy(sweep, way, chunk):
+    left = lax.broadcasted_iota(jnp.int32, (half_rows, S), 1) < half_cols
+
+    def term_copy(sweep, half, way, chunk):
         at = pl.ds(way * cap + chunk * per_chunk, per_chunk)
         return remote(
-            sends.at[sweep, at], recvs.at[sweep, at], term_send.at[sweep, way, chunk], term_recv.at[sweep, way, chunk], way
+            sends.at[sweep, half, at], recvs.at[sweep, half, at],
+            term_send.at[sweep, half, way, chunk], term_recv.at[sweep, half, way, chunk], way,
         )
 
-    def send_terms(sweep, pair):
+    def start_terms(sweep, half, pair, chunk):
+        for way in pair:
+            if_to(way, lambda way=way: term_copy(sweep, half, way, chunk).start())
+
+    def make_terms(sweep, halves, pair):
         def body(chunk, carry):
             for way in pair:
                 for r in range(per_chunk):
                     q = way * cap + chunk * per_chunk + r
-                    sends[sweep, q] = product(q).astype(jnp.bfloat16)
-            for way in pair:
-                if_to(way, lambda way=way: term_copy(sweep, way, chunk).start())
+                    block, cluster = table_s[0, q], table_s[1, q]
+                    top = jnp.dot(blocks[block, :half_rows], rounded[cluster], preferred_element_type=jnp.float32)
+                    low = jnp.dot(blocks[block, half_rows:], crossed[cluster], preferred_element_type=jnp.float32)
+                    for half in halves:
+                        packed = jnp.where(left, top, low) if half == 0 else jnp.where(left, low, top)
+                        sends[sweep, half, q] = packed.astype(jnp.bfloat16)
+            start_terms(sweep, halves[0], pair, chunk)
             return carry
 
         lax.fori_loop(0, chunks, body, 0)
+        for half in halves[1:]:
+            for chunk in range(chunks):
+                start_terms(sweep, half, pair, chunk)
+
+    def product(q):
+        return jnp.dot(blocks[table_s[0, q]], rounded[table_s[1, q]], preferred_element_type=jnp.float32)
 
     def stay():
+        acc[...] = jnp.zeros(acc.shape, jnp.float32)
+
         def group(g, carry):
             def body(t, carry):
                 at = t * unroll
@@ -232,30 +262,51 @@
 
         lax.fori_loop(0, groups, group, 0)
 
-    def receive(sweep, pair):
+    def receive(sweep, half, pair):
         def body(chunk, carry):
             for way in pair:
                 def scan(way=way):
-                    term_copy(sweep, way, chunk).wait_recv()
+                    term_copy(sweep, half, way, chunk).wait_recv()
                     for r in range(per_chunk):
                         n = chunk * per_chunk + r
                         held = jnp.where(table_in_s[way, 2, way * cap + n] != 0, arrived[way, n], 0.0)
-                        arrived[way, n + 1] = recvs[sweep, way * cap + n].astype(jnp.float32) + held
+                        arrived[way, n + 1] = recvs[sweep, half, way * cap + n].astype(jnp.float32) + held
 
                 if_from(way, scan)
             return carry
 
         lax.fori_loop(0, chunks, body, 0)
 
-    def taken(way, c):
-        return arrived[way, table_in_s[way, 3, way * clusters + c]]
+    def finish(sweep, half):
+        receive(sweep, half, (2, 3))
+        receive(sweep, half, (0, 1))
+        final = sweep == SWEEPS - 1
+
+        def body(c, carry):
+            got = sum(arrived[way, table_in_s[way, 3, way * clusters + c]] for way in range(4))
+            for n, came in enumerate((got, pltpu.roll(got, half_cols, 1))):
+                part = slice(n * half_rows, (n + 1) * half_rows)
+                at = pl.ds(pl.multiple_of(c * P_SIZE + n * half_rows, half_rows), half_rows)
+                value = emission[c, part].astype(jnp.float32) + refl[at, :] * (acc[c, part] + came)
+                if final:
+                    rad[c, part] = value if half == 0 else jnp.where(left, rad[c, part], value)
+                    turned_value = jnp.transpose(value)[half * half_cols : (half + 1) * half_cols]
+                    final_t[half * half_cols : (half + 1) * half_cols, at] = turned_value.astype(jnp.bfloat16)
+                else:
+                    if half == 1:
+                        value = jnp.where(left, rounded[c, part].astype(jnp.float32), value)
+                    rounded[c, part] = value.astype(jnp.bfloat16)
+                    crossed[c, part] = pltpu.roll(value, half_cols, 1).astype(jnp.bfloat16)
+            return carry
+
+        lax.fori_loop(0, clusters, body, 0)
 
     tile = 16
     block_rows = 8 * tile
     columns = 3 * sensors // 128
     per_wide = wide // 128
 
-    def sensor_weights(first, count):
+    def sensor_weights(first, end):
         near = lax.broadcasted_iota(jnp.int32, (tile, 128), 0)
 
         def column(n, carry):
@@ -283,72 +334,92 @@
             lax.fori_loop(0, rows // block_rows, body, 0)
             return carry
 
-        lax.fori_loop(first, first + count, column, 0)
-
-    def sweep_body(sweep, carry):
-        send_terms(sweep, (0, 1))
-        send_terms(sweep, (2, 3))
-        acc[...] = jnp.zeros(acc.shape, jnp.float32)
-        stay()
-        sensor_weights(sweep * (columns // SWEEPS), columns // SWEEPS)
-        receive(sweep, (2, 3))
-
-        def add_x(c, carry):
-            acc[c] += taken(2, c) + taken(3, c)
-            return carry
-
-        lax.fori_loop(0, clusters, add_x, 0)
-        receive(sweep, (0, 1))
-
-        def finish(c, carry):
-            at = pl.ds(pl.multiple_of(c * P_SIZE, P_SIZE), P_SIZE)
-            incoming = acc[c] + taken(0, c) + taken(1, c)
-            value = emission[c].astype(jnp.float32) + refl[at, :] * incoming
-            rounded[c] = value.astype(jnp.bfloat16)
-            rad[c] = value
-            final_t[:, at] = jnp.transpose(value).astype(jnp.bfloat16)
-            return carry
-
-        lax.fori_loop(0, clusters, finish, 0)
-        return carry
-
-    lax.fori_loop(0, SWEEPS, sweep_body, 0)
-
+        lax.fori_loop(first, end, column, 0)
+
+    def sum_copy(half, way, piece):
+        return remote(
+            sum_send.at[way, half, piece], sum_recv.at[way, half, piece],
+            sum_ssem.at[half, way, piece], sum_rsem.at[half, way, piece], way,
+        )
+
+    def sums(half, part, piece):
+        mine = final_t[half * half_cols : (half + 1) * half_cols, :]
+        return jnp.dot(mine, sensor_w[part * pieces + piece], preferred_element_type=jnp.float32)
+
+    def send_sums(half):
+        for piece in range(pieces):
+            for part in range(2):
+                way = 1 - part
+                sum_send[way, half, piece] = sums(half, part, piece).astype(jnp.bfloat16)
+                if_to(way, lambda: sum_copy(half, way, piece).start())
+        for piece in range(pieces):
+            sum_own[piece, half * half_cols : (half + 1) * half_cols] = sums(half, 2, piece)
+
+    def take_sums(half):
+        part = slice(half * half_cols, (half + 1) * half_cols)
+        for piece in range(pieces):
+            for way in range(2):
+                if_from(way, lambda: sum_copy(half, way, piece).wait_recv())
+            sum_own[piece, part] += sum_recv[0, half, piece].astype(jnp.float32) + sum_recv[1, half, piece].astype(
+                jnp.float32
+            )
+
+    assert SWEEPS == 2
+    make_terms(0, (0, 1), (0, 1))
+    make_terms(0, (0, 1), (2, 3))
+    stay()
+    sensor_weights(0, columns // 4)
+    finish(0, 0)
+    make_terms(1, (0,), (0, 1))
+    make_terms(1, (0,), (2, 3))
+    sensor_weights(columns // 4, columns)
+    finish(0, 1)
+    make_terms(1, (1,), (0, 1))
+    make_terms(1, (1,), (2, 3))
+    stay()
+    finish(1, 0)
+    send_sums(0)
+    finish(1, 1)
     write = pltpu.make_async_copy(rad, rad_hbm, load_sem.at[0])
     write.start()
-
-    def sum_copy(way, piece):
-        return remote(
-            sum_send.at[way, piece], sum_recv.at[way, piece], sum_ssem.at[way, piece], sum_rsem.at[way, piece], way
-        )
-
-    def sums(part, piece):
-        return jnp.dot(final_t[...], sensor_w[part * pieces + piece], preferred_element_type=jnp.float32)
-
-    for piece in range(pieces):
-        for part in range(2):
-            way = 1 - part
-            sum_send[way, piece] = sums(part, piece).astype(jnp.bfloat16)
-            if_to(way, lambda: sum_copy(way, piece).start())
-    for piece in range(pieces):
-        sum_own[piece] = sums(2, piece)
-    for piece in range(pieces):
-        for way in range(2):
-            if_from(way, lambda: sum_copy(way, piece).wait_recv())
-        total = sum_own[piece] + sum_recv[0, piece].astype(jnp.float32) + sum_recv[1, piece].astype(jnp.float32)
-        values[piece * wide : (piece + 1) * wide, :] = jnp.transpose(total)
-
+    send_sums(1)
+    take_sums(0)
+    take_sums(1)
     write.wait()
+
     for way in range(4):
-        if_to(way, lambda way=way: table_send(way).wait_send())
+        if_to(way, lambda: table_send(way).wait_send())
         for sweep in range(SWEEPS):
-            for chunk in range(chunks):
-                if_to(way, lambda: term_copy(sweep, way, chunk).wait_send())
+            for half in range(2):
+                for chunk in range(chunks):
+                    if_to(way, lambda: term_copy(sweep, half, way, chunk).wait_send())
     for way in range(2):
-        if_to(way, lambda way=way: cell_send(way).wait_send())
-        if_to(way, lambda way=way: weight_send(way).wait_send())
-        for piece in range(pieces):
-            if_to(way, lambda: sum_copy(way, piece).wait_send())
+        if_to(way, lambda: cell_send(way).wait_send())
+        if_to(way, lambda: weight_send(way).wait_send())
+        for half in range(2):
+            for piece in range(pieces):
+                if_to(way, lambda: sum_copy(half, way, piece).wait_send())
+
+
+def write_kernel(rad, sums, rad_out, values_out, rad_held, sums_held, values, read_sem, write_sem, *, loads):
+    share = rad.shape[0] // loads
+    reads = [pltpu.make_async_copy(sums, sums_held, read_sem.at[loads])]
+    writes = [pltpu.make_async_copy(values, values_out, write_sem.at[loads])]
+    for n in range(loads):
+        at = pl.ds(n * share, share)
+        reads.append(pltpu.make_async_copy(rad.at[at], rad_held.at[at], read_sem.at[n]))
+        writes.append(pltpu.make_async_copy(rad_held.at[at], rad_out.at[at], write_sem.at[n]))
+    for read in reads:
+        read.start()
+    for n, (read, write) in enumerate(zip(reads, writes)):
+        read.wait()
+        if n == 0:
+            wide = sums.shape[2]
+            for piece in range(sums.shape[0]):
+                values[piece * wide : (piece + 1) * wide, :] = jnp.transpose(sums_held[piece])
+        write.start()
+    for write in writes:
+        write.wait()
 
 
 def per_device(
@@ -376,11 +447,8 @@
         loads=divisor_up_to(links, 8),
     )
     full = (clusters, P_SIZE, S)
-    term = (P_SIZE, S)
+    packed = (P_SIZE // 2, S)
     chunks, pieces = dims["chunks"], sensors // wide
-
-    def as_row(x):
-        return jnp.pad(x.reshape(1, links), ((0, 0), (0, lanes - links)))
 
     vmem = pl.BlockSpec(memory_space=pltpu.VMEM)
     hbm = pl.BlockSpec(memory_space=pl.ANY)
@@ -389,22 +457,23 @@
         pltpu.VMEM((links, P_SIZE, P_SIZE), jnp.bfloat16),
         pltpu.VMEM(full, jnp.bfloat16),
         pltpu.VMEM(full, jnp.bfloat16),
+        pltpu.VMEM(full, jnp.bfloat16),
         pltpu.VMEM(full, jnp.float32),
         pltpu.VMEM((rows, S), jnp.float32),
         pltpu.VMEM(full, jnp.float32),
-        pltpu.VMEM((per_group + 1, *term), jnp.float32),
-        pltpu.VMEM((4, cap + 1, *term), jnp.float32),
-        pltpu.VMEM((SWEEPS, 4 * cap, *term), jnp.bfloat16),
-        pltpu.VMEM((SWEEPS, 4 * cap, *term), jnp.bfloat16),
+        pltpu.VMEM((per_group + 1, P_SIZE, S), jnp.float32),
+        pltpu.VMEM((4, cap + 1, *packed), jnp.float32),
+        pltpu.VMEM((SWEEPS, 2, 4 * cap, *packed), jnp.bfloat16),
+        pltpu.VMEM((SWEEPS, 2, 4 * cap, *packed), jnp.bfloat16),
         pltpu.VMEM((3, TAPS, sensors), jnp.int32),
         pltpu.VMEM((3, TAPS, sensors), jnp.float32),
         pltpu.VMEM((2, TAPS, sensors), jnp.int32),
         pltpu.VMEM((2, TAPS, sensors), jnp.float32),
         pltpu.VMEM((3 * pieces, rows, wide), jnp.bfloat16),
         pltpu.VMEM((S, rows), jnp.bfloat16),
-        pltpu.VMEM((2, pieces, S, wide), jnp.bfloat16),
-        pltpu.VMEM((2, pieces, S, wide), jnp.bfloat16),
-        pltpu.VMEM((pieces, S, wide), jnp.float32),
+        pltpu.VMEM((2, 2, pieces, S // 2, wide), jnp.bfloat16),
+        pltpu.VMEM((2, 2, pieces, S // 2, wide), jnp.bfloat16),
+        pltpu.VMEM((3, 1, lanes), jnp.int32),
         pltpu.VMEM((8, lanes), jnp.int32),
         pltpu.VMEM((4, 8, lanes), jnp.int32),
         pltpu.SMEM((8, lanes), jnp.int32),
@@ -413,29 +482,44 @@
         dma((2,)),
         dma((3, 4)),
         dma((3, 4)),
-        dma((SWEEPS, 4, chunks)),
-        dma((SWEEPS, 4, chunks)),
-        dma((2, pieces)),
-        dma((2, pieces)),
+        dma((SWEEPS, 2, 4, chunks)),
+        dma((SWEEPS, 2, 4, chunks)),
+        dma((2, 2, pieces)),
+        dma((2, 2, pieces)),
     ]
-    radiosity, values = pl.pallas_call(
+    radiosity, sums = pl.pallas_call(
         functools.partial(fused_kernel, dims=dims),
-        out_shape=[jax.ShapeDtypeStruct(full, jnp.float32), jax.ShapeDtypeStruct((sensors, S), jnp.float32)],
+        out_shape=[jax.ShapeDtypeStruct(full, jnp.float32), jax.ShapeDtypeStruct((pieces, S, wide), jnp.float32)],
         in_specs=[vmem] * 6 + [hbm] * 2,
         out_specs=[hbm, vmem],
         scratch_shapes=scratch,
         compiler_params=pltpu.CompilerParams(collective_id=0, has_side_effects=True, vmem_limit_bytes=62 * 2**20),
         name="radiosity",
     )(
-        as_row(link_target[:, 0]),
-        as_row(link_slot),
-        as_row(link_source),
+        link_target[:, 0].reshape(1, links),
+        link_slot.reshape(1, links),
+        link_source.reshape(1, links),
         sensor_cell.T,
         sensor_weight.T,
         reflectance.reshape(rows // 128, 128),
         emission.reshape(full),
         link_blocks,
     )
+    loads = divisor_up_to(clusters, 6)
+    radiosity, values = pl.pallas_call(
+        functools.partial(write_kernel, loads=loads),
+        out_shape=[jax.ShapeDtypeStruct(full, jnp.float32), jax.ShapeDtypeStruct((sensors, S), jnp.float32)],
+        in_specs=[hbm] * 2,
+        out_specs=[hbm] * 2,
+        scratch_shapes=[
+            pltpu.VMEM(full, jnp.float32),
+            pltpu.VMEM((pieces, S, wide), jnp.float32),
+            pltpu.VMEM((sensors, S), jnp.float32),
+            dma((loads + 1,)),
+            dma((loads + 1,)),
+        ],
+        name="write",
+    )(radiosity, sums)
     return radiosity.reshape(rows, S), values
 
 

time: 83.1 us -> 75.3 us (0.906)
  local copies, waits for them, and re-layouts: 7.16 us -> 0 us
    pad x3 -> x0, local copies, waits for them, and re-layouts: 3.76 us -> none  [as_row(): return jnp.pad(x.reshape(1, links), ((0, 0), (0, lanes - links)))]
    unnamed x4 -> x0, local copies, waits for them, and re-layouts: 3.4 us -> none
    pallas_call x1, Pallas kernels: 75 us -> 71.9 us  [per_device(): pl.pallas_call(functools.partial(fused_kernel, dims=dims), out_shape=[jax...]
    pallas_call x0 -> x1, Pallas kernels: none -> 2.42 us  [per_device(): pl.pallas_call(functools.partial(write_kernel, loads=loads), out_shape=[j...]
where the time goes in v1:
time: 75.3 us; the launch traced here: 74.9 us
  Pallas kernels  74.3 us (99%)
    pallas_call x1, Pallas kernels, per_device(): pl.pallas_call(functools.partial(fused_kernel, dims=dims), out_shape=[jax...  71.9 us
    pallas_call x1, Pallas kernels, per_device(): pl.pallas_call(functools.partial(write_kernel, loads=loads), out_shape=[j...  2.42 us

profile of v1, /device:TPU:18, one launch (start us, length us, event | category | flops | bytes accessed | tf_op | source)
XLA Modules:
  0.0 74.9 jit_solution(5404070169993362433)
XLA Ops:
  0.6 71.9 %radiosity.1 = (f32[12,256,128]{2,1,0:T(8,128)}, f32[2,128,256]{2,1,0:T(8,128)}) custom-call(s32[1,144]{1,0:T(1,128)} %bitcast.12, s32[1,144]{1,0:T(1,128)} %bitcast.13, s32[1,144]{1,0:T(1,128)} %bitcast.14, s32[8,512]{1,0:T(8,128)} %bitcast.9, f32[8,512]{1,0:T(8,128)} %bitcast.10, f32[24,128]{1,0:T(8,128)} %bitcast.11, bf16[12,256,128]{2,1,0:T(8,128)(2,1)} %bitcast.8, ...), custom_call_target="tpu_custom_call" | custom-call | tf_op jit(solution)/shard_map/radiosity/pallas_call | solution.py:490
  72.5 2.4 %write.1 = (f32[12,256,128]{2,1,0:T(8,128)}, f32[512,128]{1,0:T(8,128)}) custom-call(f32[12,256,128]{2,1,0:T(8,128)} %get-tuple-element.6.rad, f32[2,128,256]{2,1,0:T(8,128)} %get-tuple-element.7.sums), custom_call_target="tpu_custom_call" | custom-call | tf_op jit(solution)/shard_map/write/pallas_call | solution.py:509

commit v2 on v1

--- a/solution.py
+++ b/solution.py
@@ -80,6 +80,7 @@
     blocks, emission, rounded, crossed, rad, refl, acc, running, arrived, sends, recvs, item_cell, item_weight, from_cell,
     from_weight, sensor_w, final_t, sum_send, sum_recv, link_rows, table, table_in, table_s, table_in_s,
     load_sem, table_sem, small_send, small_recv, term_send, term_recv, sum_ssem, sum_rsem,
+    passing, hop_send, hop_recv, pass_send,
     *, dims,
 ):
     clusters, cap, per_group, groups = dims["clusters"], dims["cap"], dims["per_group"], dims["groups"]
@@ -127,6 +128,10 @@
     barrier = pltpu.get_barrier_semaphore()
     for way in range(4):
         if_to(way, lambda way=way: pl.semaphore_signal(barrier, 1, device_id=there(way)[1], device_id_type=MESH))
+    for two in (-2, 2):
+        pl.when((j + two >= 0) & (j + two < n_gy))(
+            lambda two=two: pl.semaphore_signal(barrier, 1, device_id=(i, j + two), device_id_type=MESH)
+        )
 
     link_rows[...] = jnp.zeros(link_rows.shape, jnp.int32)
     for n, link in enumerate((target, slot, source)):
@@ -135,7 +140,8 @@
     table_copy = pltpu.make_async_copy(table, table_s, table_sem.at[0])
     table_copy.start()
 
-    pl.semaphore_wait(barrier, sum(jnp.where(there(way)[0], 1, 0) for way in range(4)))
+    further = jnp.where(j >= 2, 1, 0) + jnp.where(j + 2 < n_gy, 1, 0)
+    pl.semaphore_wait(barrier, further + sum(jnp.where(there(way)[0], 1, 0) for way in range(4)))
 
     def table_send(way):
         return remote(table, table_in.at[way], small_send.at[0, way], small_recv.at[0, way], way)
@@ -206,16 +212,59 @@
 
     left = lax.broadcasted_iota(jnp.int32, (half_rows, S), 1) < half_cols
 
-    def term_copy(sweep, half, way, chunk):
-        at = pl.ds(way * cap + chunk * per_chunk, per_chunk)
+    levels = n_gy // 2 if n_gy % 2 == 0 else 1
+    odd = j % 2
+    level, mirrored = j // 2, levels - 1 - j // 2
+    depth, passed_depth = jnp.where(odd == 1, level, mirrored), jnp.where(odd == 1, mirrored, level)
+    via = jnp.where(depth < levels - 1, (levels - 1 - depth) * cap // levels, 0)
+    passed = jnp.where(passed_depth < levels - 1, (levels - 1 - passed_depth) * cap // levels, 0)
+    cross_way = 1 - odd
+
+    def term_copy(sweep, half, way, n):
         return remote(
-            sends.at[sweep, half, at], recvs.at[sweep, half, at],
-            term_send.at[sweep, half, way, chunk], term_recv.at[sweep, half, way, chunk], way,
+            sends.at[sweep, half, way * cap + n], recvs.at[sweep, half, way * cap + n],
+            term_send.at[sweep, half, way, n], term_recv.at[sweep, half, way, n], way,
         )
 
-    def start_terms(sweep, half, pair, chunk):
-        for way in pair:
-            if_to(way, lambda way=way: term_copy(sweep, half, way, chunk).start())
+    def hop_copy(sweep, half, n):
+        return pltpu.make_async_remote_copy(
+            src_ref=sends.at[sweep, half, cross_way * cap + n], dst_ref=passing.at[sweep, half, n],
+            send_sem=hop_send.at[sweep, half, n], recv_sem=hop_recv.at[sweep, half, n],
+            device_id=(i, j + 1 - 2 * odd), device_id_type=MESH,
+        )
+
+    def pass_copy(sweep, half, n):
+        return pltpu.make_async_remote_copy(
+            src_ref=passing.at[sweep, half, n], dst_ref=recvs.at[sweep, half, odd * cap + n],
+            send_sem=pass_send.at[sweep, half, n], recv_sem=term_recv.at[sweep, half, odd, n],
+            device_id=(i, j + 2 - 4 * odd), device_id_type=MESH,
+        )
+
+    def direct(way, n):
+        goes = there(way)[0]
+        return goes if way > 1 else goes & jnp.logical_not((cross_way == way) & (n < via))
+
+    def start_direct(sweep, half, way, n):
+        pl.when(direct(way, n))(lambda: term_copy(sweep, half, way, n).start())
+
+    def start_via(sweep, half, n):
+        pl.when(n < via)(lambda: hop_copy(sweep, half, n).start())
+
+    def each_term(act):
+        def body(n, carry):
+            act(n)
+            return carry
+
+        lax.fori_loop(0, cap, body, 0)
+
+    def pass_on(sweep, half):
+        def act(n):
+            @pl.when(n < passed)
+            def _():
+                hop_copy(sweep, half, n).wait_recv()
+                pass_copy(sweep, half, n).start()
+
+        each_term(act)
 
     def make_terms(sweep, halves, pair):
         def body(chunk, carry):
@@ -228,19 +277,26 @@
                     for half in halves:
                         packed = jnp.where(left, top, low) if half == 0 else jnp.where(left, low, top)
                         sends[sweep, half, q] = packed.astype(jnp.bfloat16)
-            start_terms(sweep, halves[0], pair, chunk)
+            for r in range(per_chunk):
+                n = chunk * per_chunk + r
+                if pair == (0, 1):
+                    start_via(sweep, halves[0], n)
+                for way in pair:
+                    start_direct(sweep, halves[0], way, n)
             return carry
 
         lax.fori_loop(0, chunks, body, 0)
         for half in halves[1:]:
-            for chunk in range(chunks):
-                start_terms(sweep, half, pair, chunk)
+            if pair == (0, 1):
+                each_term(lambda n: start_via(sweep, half, n))
+            each_term(lambda n: [start_direct(sweep, half, way, n) for way in pair])
 
     def product(q):
         return jnp.dot(blocks[table_s[0, q]], rounded[table_s[1, q]], preferred_element_type=jnp.float32)
 
-    def stay():
-        acc[...] = jnp.zeros(acc.shape, jnp.float32)
+    def stay(begin, end):
+        if begin == 0:
+            acc[...] = jnp.zeros(acc.shape, jnp.float32)
 
         def group(g, carry):
             def body(t, carry):
@@ -260,15 +316,15 @@
             lax.fori_loop(0, clusters, into, 0)
             return carry
 
-        lax.fori_loop(0, groups, group, 0)
+        lax.fori_loop(begin, end, group, 0)
 
     def receive(sweep, half, pair):
         def body(chunk, carry):
             for way in pair:
                 def scan(way=way):
-                    term_copy(sweep, half, way, chunk).wait_recv()
                     for r in range(per_chunk):
                         n = chunk * per_chunk + r
+                        term_copy(sweep, half, way, n).wait_recv()
                         held = jnp.where(table_in_s[way, 2, way * cap + n] != 0, arrived[way, n], 0.0)
                         arrived[way, n + 1] = recvs[sweep, half, way * cap + n].astype(jnp.float32) + held
 
@@ -282,7 +338,9 @@
         receive(sweep, half, (0, 1))
         final = sweep == SWEEPS - 1
 
-        def body(c, carry):
+        step = dims["step"]
+
+        def one(c):
             got = sum(arrived[way, table_in_s[way, 3, way * clusters + c]] for way in range(4))
             for n, came in enumerate((got, pltpu.roll(got, half_cols, 1))):
                 part = slice(n * half_rows, (n + 1) * half_rows)
@@ -297,9 +355,13 @@
                         value = jnp.where(left, rounded[c, part].astype(jnp.float32), value)
                     rounded[c, part] = value.astype(jnp.bfloat16)
                     crossed[c, part] = pltpu.roll(value, half_cols, 1).astype(jnp.bfloat16)
+
+        def body(t, carry):
+            for u in range(step):
+                one(t * step + u)
             return carry
 
-        lax.fori_loop(0, clusters, body, 0)
+        lax.fori_loop(0, clusters // step, body, 0)
 
     tile = 16
     block_rows = 8 * tile
@@ -365,19 +427,25 @@
             )
 
     assert SWEEPS == 2
+    early = groups // 2
     make_terms(0, (0, 1), (0, 1))
     make_terms(0, (0, 1), (2, 3))
-    stay()
+    stay(0, early)
+    pass_on(0, 0)
+    stay(early, groups)
     sensor_weights(0, columns // 4)
     finish(0, 0)
     make_terms(1, (0,), (0, 1))
     make_terms(1, (0,), (2, 3))
+    pass_on(0, 1)
     sensor_weights(columns // 4, columns)
     finish(0, 1)
     make_terms(1, (1,), (0, 1))
     make_terms(1, (1,), (2, 3))
-    stay()
+    pass_on(1, 0)
+    stay(0, groups)
     finish(1, 0)
+    pass_on(1, 1)
     send_sums(0)
     finish(1, 1)
     write = pltpu.make_async_copy(rad, rad_hbm, load_sem.at[0])
@@ -387,12 +455,17 @@
     take_sums(1)
     write.wait()
 
+    for sweep in range(SWEEPS):
+        for half in range(2):
+            def close(n):
+                for way in range(4):
+                    pl.when(direct(way, n))(lambda: term_copy(sweep, half, way, n).wait_send())
+                pl.when(n < via)(lambda: hop_copy(sweep, half, n).wait_send())
+                pl.when(n < passed)(lambda: pass_copy(sweep, half, n).wait_send())
+
+            each_term(close)
     for way in range(4):
         if_to(way, lambda: table_send(way).wait_send())
-        for sweep in range(SWEEPS):
-            for half in range(2):
-                for chunk in range(chunks):
-                    if_to(way, lambda: term_copy(sweep, half, way, chunk).wait_send())
     for way in range(2):
         if_to(way, lambda: cell_send(way).wait_send())
         if_to(way, lambda: weight_send(way).wait_send())
@@ -444,11 +517,11 @@
     dims = dict(
         links=links, rows=rows, clusters=clusters, sensors=sensors, cap=cap, groups=groups, per_group=per_group,
         lanes=lanes, wide=wide, unroll=divisor_up_to(per_group, 12), chunks=3 if cap % 3 == 0 else 1,
-        loads=divisor_up_to(links, 8),
+        loads=divisor_up_to(links, 8), step=divisor_up_to(clusters, 3),
     )
     full = (clusters, P_SIZE, S)
     packed = (P_SIZE // 2, S)
-    chunks, pieces = dims["chunks"], sensors // wide
+    pieces = sensors // wide
 
     vmem = pl.BlockSpec(memory_space=pltpu.VMEM)
     hbm = pl.BlockSpec(memory_space=pl.ANY)
@@ -482,10 +555,14 @@
         dma((2,)),
         dma((3, 4)),
         dma((3, 4)),
-        dma((SWEEPS, 2, 4, chunks)),
-        dma((SWEEPS, 2, 4, chunks)),
+        dma((SWEEPS, 2, 4, cap)),
+        dma((SWEEPS, 2, 4, cap)),
         dma((2, 2, pieces)),
         dma((2, 2, pieces)),
+        pltpu.VMEM((SWEEPS, 2, cap, *packed), jnp.bfloat16),
+        dma((SWEEPS, 2, cap)),
+        dma((SWEEPS, 2, cap)),
+        dma((SWEEPS, 2, cap)),
     ]
     radiosity, sums = pl.pallas_call(
         functools.partial(fused_kernel, dims=dims),

time: 75.3 us -> 72.6 us (0.964)
  Pallas kernels: 74.3 us -> 71.2 us
    pallas_call x1, Pallas kernels: 71.9 us -> 68.8 us  [per_device(): pl.pallas_call(functools.partial(fused_kernel, dims=dims), out_shape=[jax...]
where the time goes in v2:
time: 72.6 us; the launch traced here: 71.9 us
  Pallas kernels  71.2 us (98%)
    pallas_call x1, Pallas kernels, per_device(): pl.pallas_call(functools.partial(fused_kernel, dims=dims), out_shape=[jax...  68.8 us
    pallas_call x1, Pallas kernels, per_device(): pl.pallas_call(functools.partial(write_kernel, loads=loads), out_shape=[j...  2.42 us

profile of v2, /device:TPU:18, one launch (start us, length us, event | category | flops | bytes accessed | tf_op | source)
XLA Modules:
  0.0 71.9 jit_solution(17551580115061273748)
XLA Ops:
  0.6 68.8 %radiosity.1 = (f32[12,256,128]{2,1,0:T(8,128)}, f32[2,128,256]{2,1,0:T(8,128)}) custom-call(s32[1,144]{1,0:T(1,128)} %bitcast.12, s32[1,144]{1,0:T(1,128)} %bitcast.13, s32[1,144]{1,0:T(1,128)} %bitcast.14, s32[8,512]{1,0:T(8,128)} %bitcast.9, f32[8,512]{1,0:T(8,128)} %bitcast.10, f32[24,128]{1,0:T(8,128)} %bitcast.11, bf16[12,256,128]{2,1,0:T(8,128)(2,1)} %bitcast.8, ...), custom_call_target="tpu_custom_call" | custom-call | tf_op jit(solution)/shard_map/radiosity/pallas_call | solution.py:567
  69.4 2.4 %write.1 = (f32[12,256,128]{2,1,0:T(8,128)}, f32[512,128]{1,0:T(8,128)}) custom-call(f32[12,256,128]{2,1,0:T(8,128)} %get-tuple-element.6.rad, f32[2,128,256]{2,1,0:T(8,128)} %get-tuple-element.7.sums), custom_call_target="tpu_custom_call" | custom-call | tf_op jit(solution)/shard_map/write/pallas_call | solution.py:586
